TPU v7x, 32 devices: a whole 2x2x4 slice. The times are simulated.
32 devices in a mesh: row: 4 (over y, x), col: 8 (over z, core).
Axes of the slice: x: 2, y: 2, z: 4, core: 2. Of those that a mesh axis runs over, the one named last changes fastest.
Arguments:
- tiles: bfloat16 [4, 8, 128, 128, 128], P('row', 'col'), may hold values from 0 to 0.31
- block_rows: int32 [4, 8, 128], P('row', 'col'), may hold values from 0 to 63, as said below
- block_cols: int32 [4, 8, 128], P('row', 'col'), may hold values from 0 to 127
- counts: int32 [4, 8], P('row', 'col'), may hold values from 1 to 128, as said below
- seeds: int32 [8, 65536], P(None, ('col', 'row')), may hold values from 1 to 999
Outputs:
- vectors_out: float32 [8, 65536], P(None, ('col', 'row'))
- deltas: float32 [4, 8], replicated
Inputs may be any that keep to these rules, and one draw needn't show every extreme that they name: `counts`: each entry is 1, a half, a quarter or an eighth of 128 (at least 1); some device is full in every draw. On each device, among the values of block_rows (over all 128 slots) that share one quotient by 16, at most 4 are distinct; on a device whose count is 128, some quotient has exactly 4 distinct values among its tiles.
All inputs are finite; a program needn't handle non-finite values.
Results may differ from a plain program's by a relative error of at most 0.00061.
Values may be sent and summed in bfloat16 or wider, within the bound.
A program may use at most 64 MiB of HBM per device.

v0:
```python
import jax
import jax.numpy as jnp
from jax import lax
from jax.sharding import PartitionSpec as P

BLOCK = 128
TILE_BLOCK = 32
ITERS = 4
ROW_CAP = 4


def apply_tiles(partial_value, gathered, panel_block, target_block, cols_block, weight):
    taken_rows = gathered[cols_block]
    product = jnp.einsum(
        "tkc,trc->tkr", taken_rows, panel_block, preferred_element_type=jnp.float32
    )
    return partial_value.at[target_block].add(product * weight[:, None, None])


def on_device(tiles, block_rows, block_cols, counts, seeds):
    panels = tiles[0, 0]
    rows_local = block_rows[0, 0]
    cols_local = block_cols[0, 0]
    count_here = counts[0, 0]
    vectors = seeds.shape[0]
    piece_len = seeds.shape[1]
    piece_blocks = piece_len // BLOCK
    row_count = lax.axis_size("row")
    total_nodes = piece_len * row_count * lax.axis_size("col")
    row_span = row_count * piece_blocks
    tile_total = panels.shape[0]
    lane_index = jnp.arange(TILE_BLOCK, dtype=jnp.int32)
    tile_index = jnp.arange(tile_total, dtype=jnp.int32)
    live_flag = tile_index < count_here
    live_mask = live_flag.astype(jnp.float32)
    block_index = jnp.arange(row_span, dtype=jnp.int32)
    hits = (rows_local[None, :] == block_index[:, None]) & live_flag[None, :]
    present = jnp.max(hits.astype(jnp.int32), axis=1).reshape(row_count, piece_blocks)
    rank = jnp.cumsum(present, axis=1) - present
    owner_index = jnp.arange(row_count, dtype=jnp.int32)
    block_slot = (owner_index[:, None] * ROW_CAP + rank).reshape(row_span)
    slot_total = row_count * ROW_CAP
    matched = jnp.where(rows_local[:, None] == block_index[None, :], block_slot[None, :], 0)
    targets = jnp.minimum(jnp.sum(matched, axis=1), slot_total - 1)
    slot_index = jnp.arange(ROW_CAP, dtype=jnp.int32)
    offset_index = jnp.arange(piece_blocks, dtype=jnp.int32)
    matches = (present[:, None, :] == 1) & (rank[:, None, :] == slot_index[None, :, None])
    slot_ids = jnp.sum(jnp.where(matches, offset_index[None, None, :], 0), axis=2)
    row_total = jnp.sum(panels, axis=2, dtype=jnp.float32) * live_mask[:, None]
    degree_part = (
        jnp.zeros((slot_total, 1, BLOCK), jnp.float32).at[targets].add(row_total[:, None, :])
    )
    seed_float = seeds.astype(jnp.float32)
    seed_total = lax.psum(jnp.sum(seed_float, axis=1), ("row", "col"))
    current = (
        (total_nodes * seed_float / seed_total[:, None])
        .reshape(vectors, piece_blocks, BLOCK)
        .transpose(1, 0, 2)
    )
    empty_sum = jnp.zeros((slot_total, vectors, BLOCK), jnp.float32)
    deltas = []
    divisor = None
    owner_table = None
    for iteration in range(ITERS):
        current_half = current.astype(jnp.bfloat16)
        gathered = lax.all_gather(current_half, "col", axis=0, tiled=True)

        def advance(block_at, partial_value):
            begin_at = block_at * TILE_BLOCK
            weight = (begin_at + lane_index < count_here).astype(jnp.float32)
            return apply_tiles(
                partial_value,
                gathered,
                lax.dynamic_slice_in_dim(panels, begin_at, TILE_BLOCK, 0),
                lax.dynamic_slice_in_dim(targets, begin_at, TILE_BLOCK, 0),
                lax.dynamic_slice_in_dim(cols_local, begin_at, TILE_BLOCK, 0),
                weight,
            )

        partial_value = lax.fori_loop(
            0, (count_here + TILE_BLOCK - 1) // TILE_BLOCK, advance, empty_sum
        )
        shaped = partial_value.reshape(row_count, ROW_CAP, vectors, BLOCK)
        if iteration == 0:
            degree_shaped = degree_part.reshape(row_count, ROW_CAP, 1, BLOCK)
            incoming, degree_in, received_ids = (
                lax.all_to_all(shaped, "row", split_axis=0, concat_axis=0, tiled=True),
                lax.all_to_all(degree_shaped, "row", split_axis=0, concat_axis=0, tiled=True),
                lax.all_to_all(slot_ids, "row", split_axis=0, concat_axis=0, tiled=True),
            )
            block_index_own = jnp.arange(piece_blocks, dtype=jnp.int32)
            owner_table = (received_ids.reshape(-1)[None, :] == block_index_own[:, None]).astype(
                jnp.float32
            )
            degree_piece = jnp.dot(
                owner_table,
                degree_in.reshape(row_count * ROW_CAP, BLOCK),
                precision=lax.Precision.HIGHEST,
                preferred_element_type=jnp.float32,
            )
            divisor = 1.0 + degree_piece.reshape(piece_blocks, 1, BLOCK)
        else:
            incoming = lax.all_to_all(shaped, "row", split_axis=0, concat_axis=0, tiled=True)
        summed = jnp.dot(
            owner_table,
            incoming.reshape(row_count * ROW_CAP, vectors * BLOCK),
            precision=lax.Precision.HIGHEST,
            preferred_element_type=jnp.float32,
        ).reshape(piece_blocks, vectors, BLOCK)
        raw_next = (summed + current) / divisor
        local_total = jnp.sum(raw_next, axis=(0, 2))
        totals = lax.psum(local_total, ("row", "col"))
        updated = total_nodes * raw_next / totals[None, :, None]
        deltas.append(lax.pmax(jnp.max(jnp.abs(updated - current), axis=(0, 2)), ("row", "col")))
        current = updated
    vectors_out = current.transpose(1, 0, 2).reshape(vectors, piece_len)
    return (vectors_out, jnp.stack(deltas))


def solution(mesh):
    placed = (
        P("row", "col", None, None, None),
        P("row", "col", None),
        P("row", "col", None),
        P("row", "col"),
        P(None, ("col", "row")),
    )
    return jax.shard_map(
        on_device,
        mesh=mesh,
        in_specs=placed,
        out_specs=(P(None, ("col", "row")), P()),
        check_vma=False,
    )
```

profile of v0, /device:TPU:0, one launch (start us, length us, event | category | flops | bytes accessed | tf_op | source)
XLA Modules:
  0.0 454.9 jit_solution(6785953493534906902)
XLA Ops:
  1.3 0.8 convert_reduce_fusion.2
  2.4 0.7 select_reduce_fusion.1
  3.1 5.2 %all-to-all-start = ((s32[4,1,4]{2,1,0:T(1,128)}), s32[4,1,4]{2,1,0:T(1,128)S(1)}, u32[]{:S(2)}, u32[]{:S(2)}) async-start(s32[4,1,4]{2,1,0:T(1,128)} %bitcast.3), calls=%async_computation | async-start | bytes 4096 | tf_op jit(solution)/shard_map/all_to_all | solution.py:89
  8.6 0.7 select_reduce_fusion
  9.3 1.0 convert_reduce_fusion.1
  10.3 40.9 %psum.35 = f32[8]{0:T(128)S(1)} all-reduce(f32[8]{0:T(128)S(1)} %convert_reduce_fusion.1), channel_id=1, replica_groups=mesh['row'=4,'col'=8] {'row','col'}, use_global_device_ids=true, to_apply=%region_5.6 | all-reduce | flops 8 | bytes 64 | tf_op jit(solution)/shard_map/psum | solution.py:54
  51.2 0.9 divide_bitcast_fusion.1
  52.2 14.3 %all_gather.12 = bf16[128,8,128]{2,0,1:T(8,128)(2,1)S(1)} all-gather(bf16[16,8,128]{2,0,1:T(8,128)(2,1)S(1)} %bitcast.214), channel_id=1, replica_groups=mesh['row'=4,'col'=8] {'col'}, dimensions={0}, use_global_device_ids=true | all-gather | bytes 294912 | tf_op jit(solution)/shard_map/all_gather | solution.py:66
  66.6 3.4 convert_reduce_fusion
  70.0 1.6 scatter_custom_fusion.4
  71.6 3.5 all-to-all-start.2
  75.8 28.4 %while.44 = (s32[]{:T(128)}, f32[16,8,128]{2,1,0:T(8,128)}, s32[]{:T(128)}, s32[128]{0:T(128)S(1)}, s32[128]{0:T(128)S(1)}, /*index=5*/bf16[128,8,128]{2,1,0:T(8...) while((s32[]{:T(128)}, f32[16,8,128]{2,1,0:T(8,128)}, ...), condition=%wide.region_8.9_spmd.clone, body=%wide.region_6.8_spmd.clone.sunk | while | flops 8455462 | bytes 1774899 | solution.py:80
  77.2 1.9 convolution_multiply_fusion.8
  79.0 3.9 scatter_fusion
  84.2 1.9 convolution_multiply_fusion.8
  86.1 3.9 scatter_fusion
  91.3 1.9 convolution_multiply_fusion.8
  93.2 3.9 scatter_fusion
  98.4 1.9 convolution_multiply_fusion.8
  100.3 3.9 scatter_fusion
  104.7 0.7 reduce.3
  105.5 3.3 all-to-all-start.1
  108.9 4.7 %all-to-all-done.1 = f32[4,4,8,128]{3,2,1,0:T(8,128)S(1)} async-done(((f32[4,4,8,128]{3,2,1,0:T(8,128)}), f32[4,4,8,128]{3,2,1,0:T(8,128)S(1)}, u32[]{:S(2)}, u32[]{:S(2)}) %all-to-all-start.1) | async-done | bytes 65568 | tf_op jit(solution)/shard_map/all_to_all | solution.py:87
  113.9 38.4 %psum.36 = f32[8]{0:T(128)S(1)} all-reduce(f32[8]{0:T(128)S(1)} %get-tuple-element.490), channel_id=1, replica_groups=mesh['row'=4,'col'=8] {'row','col'}, use_global_device_ids=true, to_apply=%region_12.13 | all-reduce | flops 8 | bytes 64 | tf_op jit(solution)/shard_map/psum | solution.py:112
  152.3 14.2 %all_gather.13 = bf16[128,8,128]{2,0,1:T(8,128)(2,1)S(1)} all-gather(bf16[16,8,128]{2,0,1:T(8,128)(2,1)S(1)} %get-tuple-element.480), channel_id=1, replica_groups=mesh['row'=4,'col'=8] {'col'}, dimensions={0}, use_global_device_ids=true | all-gather | bytes 294912 | tf_op jit(solution)/shard_map/all_gather | solution.py:66
  167.3 28.4 %while.45 = (s32[]{:T(128)}, f32[16,8,128]{2,1,0:T(8,128)}, s32[]{:T(128)}, s32[128]{0:T(128)S(1)}, s32[128]{0:T(128)S(1)}, /*index=5*/bf16[128,8,128]{2,1,0:T(8...) while((s32[]{:T(128)}, f32[16,8,128]{2,1,0:T(8,128)}, ...), condition=%wide.region_15.16_spmd.clone, body=%wide.region_13.15_spmd.clone.sunk | while | flops 8455462 | bytes 1774899 | solution.py:80
  168.7 1.9 convolution_multiply_fusion.9
  170.5 3.9 scatter_fusion.1
  175.7 1.9 convolution_multiply_fusion.9
  177.6 3.9 scatter_fusion.1
  182.8 1.9 convolution_multiply_fusion.9
  184.7 3.9 scatter_fusion.1
  189.9 1.9 convolution_multiply_fusion.9
  191.8 3.9 scatter_fusion.1
  195.7 3.5 all-to-all-start.3
  199.2 4.8 %all-to-all-done.3 = f32[4,4,8,128]{3,2,1,0:T(8,128)S(1)} async-done(((f32[4,4,8,128]{3,2,1,0:T(8,128)}), f32[4,4,8,128]{3,2,1,0:T(8,128)S(1)}, u32[]{:S(2)}, u32[]{:S(2)}) %all-to-all-start.3) | async-done | bytes 65568 | tf_op jit(solution)/shard_map/all_to_all | solution.py:103
  204.4 37.9 %psum.37 = f32[8]{0:T(128)S(1)} all-reduce(f32[8]{0:T(128)S(1)} %get-tuple-element.403), channel_id=1, replica_groups=mesh['row'=4,'col'=8] {'row','col'}, use_global_device_ids=true, to_apply=%region_17.18 | all-reduce | flops 8 | bytes 64 | tf_op jit(solution)/shard_map/psum | solution.py:112
  242.3 14.2 %all_gather.14 = bf16[128,8,128]{2,0,1:T(8,128)(2,1)S(1)} all-gather(bf16[16,8,128]{2,0,1:T(8,128)(2,1)S(1)} %get-tuple-element.478), channel_id=1, replica_groups=mesh['row'=4,'col'=8] {'col'}, dimensions={0}, use_global_device_ids=true | all-gather | bytes 294912 | tf_op jit(solution)/shard_map/all_gather | solution.py:66
  257.3 28.4 %while.46 = (s32[]{:T(128)}, f32[16,8,128]{2,1,0:T(8,128)}, s32[]{:T(128)}, s32[128]{0:T(128)S(1)}, s32[128]{0:T(128)S(1)}, /*index=5*/bf16[128,8,128]{2,1,0:T(8...) while((s32[]{:T(128)}, f32[16,8,128]{2,1,0:T(8,128)}, ...), condition=%wide.region_20.21_spmd.clone, body=%wide.region_18.20_spmd.clone.sunk | while | flops 8455462 | bytes 1774899 | solution.py:80
  258.7 1.9 convolution_multiply_fusion.10
  260.5 3.9 scatter_fusion.2
  265.8 1.9 convolution_multiply_fusion.10
  267.6 3.9 scatter_fusion.2
  272.9 1.9 convolution_multiply_fusion.10
  274.7 3.9 scatter_fusion.2
  279.9 1.9 convolution_multiply_fusion.10
  281.8 3.9 scatter_fusion.2
  285.7 3.5 all-to-all-start.4
  289.3 4.8 %all-to-all-done.4 = f32[4,4,8,128]{3,2,1,0:T(8,128)S(1)} async-done(((f32[4,4,8,128]{3,2,1,0:T(8,128)}), f32[4,4,8,128]{3,2,1,0:T(8,128)S(1)}, u32[]{:S(2)}, u32[]{:S(2)}) %all-to-all-start.4) | async-done | bytes 65568 | tf_op jit(solution)/shard_map/all_to_all | solution.py:103
  294.4 37.7 %psum.38 = f32[8]{0:T(128)S(1)} all-reduce(f32[8]{0:T(128)S(1)} %get-tuple-element.405), channel_id=1, replica_groups=mesh['row'=4,'col'=8] {'row','col'}, use_global_device_ids=true, to_apply=%region_22.23 | all-reduce | flops 8 | bytes 64 | tf_op jit(solution)/shard_map/psum | solution.py:112
  332.1 14.5 %all_gather.15 = bf16[128,8,128]{2,0,1:T(8,128)(2,1)S(1)} all-gather(bf16[16,8,128]{2,0,1:T(8,128)(2,1)S(1)} %get-tuple-element.476), channel_id=1, replica_groups=mesh['row'=4,'col'=8] {'col'}, dimensions={0}, use_global_device_ids=true | all-gather | bytes 294912 | tf_op jit(solution)/shard_map/all_gather | solution.py:66
  346.8 19.7 %while.47 = (s32[]{:T(128)}, f32[16,8,128]{2,1,0:T(8,128)S(1)}, s32[]{:T(128)}, s32[128]{0:T(128)S(1)}, s32[128]{0:T(128)S(1)}, /*index=5*/bf16[128,8,128]{2,1,0...) while((s32[]{:T(128)}, f32[16,8,128]{2,1,0:T(8,128)S(1)}, ...), condition=%wide.region_25.26_spmd.clone, body=%wide.region_23.25_spmd.clone.sunk | while | flops 8455462 | bytes 1774899 | solution.py:80
  348.2 1.9 convolution_multiply_fusion.11
  350.0 1.7 scatter_fusion.3
  353.1 1.9 convolution_multiply_fusion.11
  354.9 1.7 scatter_fusion.3
  358.0 1.9 convolution_multiply_fusion.11
  359.8 1.7 scatter_fusion.3
  362.9 1.9 convolution_multiply_fusion.11
  364.8 1.7 scatter_fusion.3
  366.5 8.2 %all_to_all.34 = f32[4,4,8,128]{3,2,1,0:T(8,128)S(1)} all-to-all(f32[4,4,8,128]{3,2,1,0:T(8,128)S(1)} %bitcast.212), channel_id=1, replica_groups=mesh['row'=4,'col'=8] {'row'}, dimensions={0} | all-to-all | bytes 131072 | tf_op jit(solution)/shard_map/all_to_all | solution.py:103
  375.0 37.6 %psum.39 = f32[8]{0:T(128)S(1)} all-reduce(f32[8]{0:T(128)S(1)} %get-tuple-element.494), channel_id=1, replica_groups=mesh['row'=4,'col'=8] {'row','col'}, use_global_device_ids=true, to_apply=%region_27.28 | all-reduce | flops 8 | bytes 64 | tf_op jit(solution)/shard_map/psum | solution.py:112
  412.9 0.7 copy.93
  413.6 40.7 %all-reduce = (f32[1,8]{1,0:T(1,128)S(1)}, f32[1,8]{1,0:T(1,128)S(1)}, f32[1,8]{1,0:T(1,128)S(1)}, f32[1,8]{1,0:T(1,128)S(1)}) all-reduce(f32[1,8]{1,0:T(1,128)S(1)} %bitcast.222, f32[1,8]{1,0:T(1,128)S(1)} %bitcast.221, f32[1,8]{1,0:T(1,128)S(1)} %bitcast.224, f32[1,8]{1,0:T(1,128)S(1)} %bitcast.223), channel_id=1, replica_groups=mesh['row'=4,'col'=8] {'row','col'}, use_global_device_ids=true, to_apply=%region_35.36 | all-reduce | flops 32 | bytes 256 | tf_op jit(solution)/shard_map/pmax | solution.py:114
  (102 shorter events, 27.5 us)
Async XLA Ops:
  0.6 75.2 %copy-start = (s32[1,1,128]{2,1,0:T(1,128)S(1)}, s32[1,1,128]{2,1,0:T(1,128)}, u32[]{:S(2)}) copy-start(s32[1,1,128]{2,1,0:T(1,128)} %param.15) | copy-start | bytes 1540
  3.1 68.5 %all-to-all-start = ((s32[4,1,4]{2,1,0:T(1,128)}), s32[4,1,4]{2,1,0:T(1,128)S(1)}, u32[]{:S(2)}, u32[]{:S(2)}) async-start(s32[4,1,4]{2,1,0:T(1,128)} %bitcast.3), calls=%async_computation | async-start | bytes 4096 | tf_op jit(solution)/shard_map/all_to_all | solution.py:89
  71.6 33.8 %all-to-all-start.2 = ((f32[4,4,1,128]{3,1,2,0:T(4,128)}), f32[4,4,1,128]{3,1,2,0:T(4,128)S(1)}, u32[]{:S(2)}, u32[]{:S(2)}) async-start(f32[4,4,1,128]{3,1,2,0:T(4,128)} %bitcast.14), calls=%async_computation.2 | async-start | bytes 16384 | tf_op jit(solution)/shard_map/all_to_all | solution.py:88
  105.5 8.1 %all-to-all-start.1 = ((f32[4,4,8,128]{3,2,1,0:T(8,128)}), f32[4,4,8,128]{3,2,1,0:T(8,128)S(1)}, u32[]{:S(2)}, u32[]{:S(2)}) async-start(f32[4,4,8,128]{3,2,1,0:T(8,128)} %bitcast.8), calls=%async_computation.1 | async-start | bytes 131072 | tf_op jit(solution)/shard_map/all_to_all | solution.py:87
  195.7 8.4 %all-to-all-start.3 = ((f32[4,4,8,128]{3,2,1,0:T(8,128)}), f32[4,4,8,128]{3,2,1,0:T(8,128)S(1)}, u32[]{:S(2)}, u32[]{:S(2)}) async-start(f32[4,4,8,128]{3,2,1,0:T(8,128)} %bitcast.16), calls=%async_computation.3 | async-start | bytes 131072 | tf_op jit(solution)/shard_map/all_to_all | solution.py:103
  285.7 8.4 %all-to-all-start.4 = ((f32[4,4,8,128]{3,2,1,0:T(8,128)}), f32[4,4,8,128]{3,2,1,0:T(8,128)S(1)}, u32[]{:S(2)}, u32[]{:S(2)}) async-start(f32[4,4,8,128]{3,2,1,0:T(8,128)} %bitcast.18), calls=%async_computation.4 | async-start | bytes 131072 | tf_op jit(solution)/shard_map/all_to_all | solution.py:103
where the time goes:
time: 458 us; the launch traced here: 455 us
  blocking collectives  298 us (65%)
  other arithmetic  76.5 us (17%)
  matrix products  31 us (7%)
  starting transfers between devices  19.1 us (4%)
  waiting for transfers between devices  14.4 us (3%)
  local copies, waits for them, and re-layouts  13.7 us (3%)
    psum x4, blocking collectives, on_device(): totals = lax.psum(local_total, ('row', 'col'))  152 us
    all_gather x4, blocking collectives, on_device(): gathered = lax.all_gather(current_half, 'col', axis=0, tiled=True)  57.1 us
    scatter-add x16, other arithmetic, apply_tiles(): return partial_value.at[target_block].add(product * weight[:, None, None])  53.6 us
    psum x1, blocking collectives, on_device(): seed_total = lax.psum(jnp.sum(seed_float, axis=1), ('row', 'col'))  40.9 us
    pmax x1, blocking collectives, on_device(): lax.pmax(jnp.max(jnp.abs(updated - current), axis=(0, 2)), ('row', 'col'))  40.7 us
    dot_general x16, matrix products, apply_tiles(): jnp.einsum('tkc,trc->tkr', taken_rows, panel_block, preferred_element_typ...  29.7 us
    all_to_all x3, waiting for transfers between devices, on_device(): lax.all_to_all(shaped, 'row', split_axis=0, concat_axis=0, tiled=True)  14.4 us
    convert_element_type x16, other arithmetic, advance(): weight = (begin_at + lane_index < count_here).astype(jnp.float32)  10.4 us
  transfers between devices with their start and end apart: 5, of which 3 were waited for; matrix products, arithmetic and copies ran while one was open for 8% of the time, Pallas kernels for 0%

commit v1 on v0

--- a/solution.py
+++ b/solution.py
@@ -63,7 +63,21 @@
     owner_table = None
     for iteration in range(ITERS):
         current_half = current.astype(jnp.bfloat16)
-        gathered = lax.all_gather(current_half, "col", axis=0, tiled=True)
+        parts_n = lax.axis_size("col")
+        parts_seen = [current_half]
+        dd = 0
+        while dd < parts_n - 1:
+            parts_seen.append(
+                lax.ppermute(
+                    parts_seen[-1], "col", [(jj, (jj + 1) % parts_n) for jj in range(parts_n)]
+                )
+            )
+            dd = dd + 1
+        gathered = jnp.roll(
+            jnp.concatenate(parts_seen[::-1], axis=0),
+            (lax.axis_index("col") + 1) * current_half.shape[0],
+            axis=0,
+        )
 
         def advance(block_at, partial_value):
             begin_at = block_at * TILE_BLOCK

time: 458 us -> 508 us (1.11)
  waiting for transfers between devices: 14.4 us -> 133 us
  blocking collectives: 298 us -> 256 us
  other arithmetic: 76.5 us -> 58.8 us
  starting transfers between devices: 19.1 us -> 12.7 us
    ppermute x0 -> x28, waiting for transfers between devices: none -> 128 us  [on_device(): lax.ppermute(parts_seen[-1], 'col', [(jj, (jj + 1) % parts_n) for jj in r...]
    all_gather x4 -> x0, blocking collectives: 57.1 us -> none  [on_device(): gathered = lax.all_gather(current_half, 'col', axis=0, tiled=True)]
    scatter-add x16, other arithmetic: 53.6 us -> 35.8 us  [apply_tiles(): return partial_value.at[target_block].add(product * weight[:, None, None])]
    all_to_all x1 -> x3, blocking collectives: 8.19 us -> 24.6 us  [on_device(): lax.all_to_all(shaped, 'row', split_axis=0, concat_axis=0, tiled=True)]
    all_to_all x3 -> x1, waiting for transfers between devices: 14.4 us -> 4.71 us  [on_device(): lax.all_to_all(shaped, 'row', split_axis=0, concat_axis=0, tiled=True)]
    all_to_all x3 -> x1, starting transfers between devices: 10.3 us -> 3.29 us  [on_device(): lax.all_to_all(shaped, 'row', split_axis=0, concat_axis=0, tiled=True)]
  transfers between devices with their start and end apart: 5 -> 31, of which waited for: 3 -> 27; matrix products, arithmetic and copies ran while one was open for 8% -> 7% of each run, Pallas kernels for 0% -> 0%
where the time goes in v1:
time: 508 us; the launch traced here: 506 us
  blocking collectives  256 us (50%)
  waiting for transfers between devices  133 us (26%)
  other arithmetic  58.8 us (12%)
  matrix products  31 us (6%)
  local copies, waits for them, and re-layouts  12.8 us (3%)
  starting transfers between devices  12.7 us (2%)
    psum x4, blocking collectives, on_device(): totals = lax.psum(local_total, ('row', 'col'))  148 us
    ppermute x28, waiting for transfers between devices, on_device(): lax.ppermute(parts_seen[-1], 'col', [(jj, (jj + 1) % parts_n) for jj in r...  128 us
    psum x1, blocking collectives, on_device(): seed_total = lax.psum(jnp.sum(seed_float, axis=1), ('row', 'col'))  42 us
    pmax x1, blocking collectives, on_device(): lax.pmax(jnp.max(jnp.abs(updated - current), axis=(0, 2)), ('row', 'col'))  41.5 us
    scatter-add x16, other arithmetic, apply_tiles(): return partial_value.at[target_block].add(product * weight[:, None, None])  35.8 us
    dot_general x16, matrix products, apply_tiles(): jnp.einsum('tkc,trc->tkr', taken_rows, panel_block, preferred_element_typ...  29.7 us
    all_to_all x3, blocking collectives, on_device(): lax.all_to_all(shaped, 'row', split_axis=0, concat_axis=0, tiled=True)  24.6 us
    convert_element_type x16, other arithmetic, advance(): weight = (begin_at + lane_index < count_here).astype(jnp.float32)  10.4 us
  transfers between devices with their start and end apart: 31, of which 27 were waited for; matrix products, arithmetic and copies ran while one was open for 7% of the time, Pallas kernels for 0%

profile of v1, /device:TPU:0, one launch (start us, length us, event | category | flops | bytes accessed | tf_op | source)
XLA Modules:
  0.0 506.3 jit_solution(15349318308590136326)
XLA Ops:
  1.6 42.0 %psum.35 = f32[8]{0:T(128)S(1)} all-reduce(f32[8]{0:T(128)S(1)} %convert_reduce_fusion.1), channel_id=1, replica_groups=mesh['row'=4,'col'=8] {'row','col'}, use_global_device_ids=true, to_apply=%region_5.6 | all-reduce | flops 8 | bytes 64 | tf_op jit(solution)/shard_map/psum | solution.py:54
  47.1 3.5 all-to-all-start
  52.0 3.4 convert_reduce_fusion
  56.0 4.9 collective-permute-done.2
  60.9 5.1 %collective-permute-done.3 = bf16[16,8,128]{2,0,1:T(8,128)(2,1)S(1)} collective-permute-done((bf16[16,8,128]{2,0,1:T(8,128)(2,1)S(1)}, bf16[16,8,128]{2,0,1:T(8,128)(2,1)S(1)}, u32[]{:S(2)}, u32[]{:S(2)}) %collective-permute-start.3) | collective-permute-done | bytes 32800 | tf_op jit(solution)/shard_map/ppermute | solution.py:71
  66.2 5.0 collective-permute-done.4
  71.2 5.1 %collective-permute-done.5 = bf16[16,8,128]{2,0,1:T(8,128)(2,1)S(1)} collective-permute-done((bf16[16,8,128]{2,0,1:T(8,128)(2,1)S(1)}, bf16[16,8,128]{2,0,1:T(8,128)(2,1)S(1)}, u32[]{:S(2)}, u32[]{:S(2)}) %collective-permute-start.5) | collective-permute-done | bytes 32800 | tf_op jit(solution)/shard_map/ppermute | solution.py:71
  78.0 4.2 all-to-all-start.2
  84.5 28.4 %while.44 = (s32[]{:T(128)}, f32[16,8,128]{2,1,0:T(8,128)}, s32[]{:T(128)}, s32[128]{0:T(128)S(1)}, s32[128]{0:T(128)S(1)}, /*index=5*/bf16[128,8,128]{2,1,0:T(8...) while((s32[]{:T(128)}, f32[16,8,128]{2,1,0:T(8,128)}, ...), condition=%wide.region_8.10_spmd.clone, body=%wide.region_6.9_spmd.clone.sunk | while | flops 8455462 | bytes 1774899 | solution.py:94
  85.9 1.9 convolution_multiply_fusion.8
  87.7 3.9 scatter_fusion
  93.0 1.9 convolution_multiply_fusion.8
  94.8 3.9 scatter_fusion
  100.1 1.9 convolution_multiply_fusion.8
  101.9 3.9 scatter_fusion
  107.1 1.9 convolution_multiply_fusion.8
  109.0 3.9 scatter_fusion
  112.9 3.3 all-to-all-start.1
  116.3 4.7 all-to-all-done.1
  121.4 36.9 %psum.36 = f32[8]{0:T(128)S(1)} all-reduce(f32[8]{0:T(128)S(1)} %get-tuple-element.491), channel_id=1, replica_groups=mesh['row'=4,'col'=8] {'row','col'}, use_global_device_ids=true, to_apply=%region_12.14 | all-reduce | flops 8 | bytes 64 | tf_op jit(solution)/shard_map/psum | solution.py:126
  158.4 5.1 %collective-permute-done.7 = bf16[16,8,128]{2,0,1:T(8,128)(2,1)S(1)} collective-permute-done((bf16[16,8,128]{2,0,1:T(8,128)(2,1)S(1)}, bf16[16,8,128]{2,0,1:T(8,128)(2,1)S(1)}, u32[]{:S(2)}, u32[]{:S(2)}) %collective-permute-start.7) | collective-permute-done | bytes 32800 | tf_op jit(solution)/shard_map/ppermute | solution.py:71
  163.5 5.1 %collective-permute-done.8 = bf16[16,8,128]{2,0,1:T(8,128)(2,1)S(1)} collective-permute-done((bf16[16,8,128]{2,0,1:T(8,128)(2,1)S(1)}, bf16[16,8,128]{2,0,1:T(8,128)(2,1)S(1)}, u32[]{:S(2)}, u32[]{:S(2)}) %collective-permute-start.8) | collective-permute-done | bytes 32800 | tf_op jit(solution)/shard_map/ppermute | solution.py:71
  168.6 5.1 %collective-permute-done.9 = bf16[16,8,128]{2,0,1:T(8,128)(2,1)S(1)} collective-permute-done((bf16[16,8,128]{2,0,1:T(8,128)(2,1)S(1)}, bf16[16,8,128]{2,0,1:T(8,128)(2,1)S(1)}, u32[]{:S(2)}, u32[]{:S(2)}) %collective-permute-start.9) | collective-permute-done | bytes 32800 | tf_op jit(solution)/shard_map/ppermute | solution.py:71
  173.8 5.1 %collective-permute-done.10 = bf16[16,8,128]{2,0,1:T(8,128)(2,1)S(1)} collective-permute-done((bf16[16,8,128]{2,0,1:T(8,128)(2,1)S(1)}, bf16[16,8,128]{2,0,1:T(8,128)(2,1)S(1)}, u32[]{:S(2)}, u32[]{:S(2)}) %collective-permute-start.10) | collective-permute-done | bytes 32800 | tf_op jit(solution)/shard_map/ppermute | solution.py:71
  178.9 5.1 %collective-permute-done.11 = bf16[16,8,128]{2,0,1:T(8,128)(2,1)S(1)} collective-permute-done((bf16[16,8,128]{2,0,1:T(8,128)(2,1)S(1)}, bf16[16,8,128]{2,0,1:T(8,128)(2,1)S(1)}, u32[]{:S(2)}, u32[]{:S(2)}) %collective-permute-start.11) | collective-permute-done | bytes 32800 | tf_op jit(solution)/shard_map/ppermute | solution.py:71
  184.1 5.1 %collective-permute-done.12 = bf16[16,8,128]{2,0,1:T(8,128)(2,1)S(1)} collective-permute-done((bf16[16,8,128]{2,0,1:T(8,128)(2,1)S(1)}, bf16[16,8,128]{2,0,1:T(8,128)(2,1)S(1)}, u32[]{:S(2)}, u32[]{:S(2)}) %collective-permute-start.12) | collective-permute-done | bytes 32800 | tf_op jit(solution)/shard_map/ppermute | solution.py:71
  189.2 5.1 %collective-permute-done.13 = bf16[16,8,128]{2,0,1:T(8,128)(2,1)S(1)} collective-permute-done((bf16[16,8,128]{2,0,1:T(8,128)(2,1)S(1)}, bf16[16,8,128]{2,0,1:T(8,128)(2,1)S(1)}, u32[]{:S(2)}, u32[]{:S(2)}) %collective-permute-start.13) | collective-permute-done | bytes 32800 | tf_op jit(solution)/shard_map/ppermute | solution.py:71
  194.8 19.7 %while.45 = (s32[]{:T(128)}, f32[16,8,128]{2,1,0:T(8,128)S(1)}, s32[]{:T(128)}, s32[128]{0:T(128)S(1)}, s32[128]{0:T(128)S(1)}, /*index=5*/bf16[128,8,128]{2,1,0...) while((s32[]{:T(128)}, f32[16,8,128]{2,1,0:T(8,128)S(1)}, ...), condition=%wide.region_15.17_spmd.clone, body=%wide.region_13.16_spmd.clone.sunk | while | flops 8455462 | bytes 1774899 | solution.py:94
  196.2 1.9 convolution_multiply_fusion.9
  201.1 1.9 convolution_multiply_fusion.9
  206.0 1.9 convolution_multiply_fusion.9
  210.9 1.9 convolution_multiply_fusion.9
  212.8 1.7 scatter_fusion.1
  214.5 8.2 %all_to_all.34 = f32[4,4,8,128]{3,2,1,0:T(8,128)S(1)} all-to-all(f32[4,4,8,128]{3,2,1,0:T(8,128)S(1)} %bitcast.217), channel_id=1, replica_groups=mesh['row'=4,'col'=8] {'row'}, dimensions={0} | all-to-all | bytes 131072 | tf_op jit(solution)/shard_map/all_to_all | solution.py:117
  223.0 36.9 %psum.37 = f32[8]{0:T(128)S(1)} all-reduce(f32[8]{0:T(128)S(1)} %get-tuple-element.404), channel_id=1, replica_groups=mesh['row'=4,'col'=8] {'row','col'}, use_global_device_ids=true, to_apply=%region_17.19 | all-reduce | flops 8 | bytes 64 | tf_op jit(solution)/shard_map/psum | solution.py:126
  260.0 5.1 %collective-permute-done.14 = bf16[16,8,128]{2,0,1:T(8,128)(2,1)S(1)} collective-permute-done((bf16[16,8,128]{2,0,1:T(8,128)(2,1)S(1)}, bf16[16,8,128]{2,0,1:T(8,128)(2,1)S(1)}, u32[]{:S(2)}, u32[]{:S(2)}) %collective-permute-start.14) | collective-permute-done | bytes 32800 | tf_op jit(solution)/shard_map/ppermute | solution.py:71
  265.1 5.1 %collective-permute-done.15 = bf16[16,8,128]{2,0,1:T(8,128)(2,1)S(1)} collective-permute-done((bf16[16,8,128]{2,0,1:T(8,128)(2,1)S(1)}, bf16[16,8,128]{2,0,1:T(8,128)(2,1)S(1)}, u32[]{:S(2)}, u32[]{:S(2)}) %collective-permute-start.15) | collective-permute-done | bytes 32800 | tf_op jit(solution)/shard_map/ppermute | solution.py:71
  270.3 5.1 %collective-permute-done.16 = bf16[16,8,128]{2,0,1:T(8,128)(2,1)S(1)} collective-permute-done((bf16[16,8,128]{2,0,1:T(8,128)(2,1)S(1)}, bf16[16,8,128]{2,0,1:T(8,128)(2,1)S(1)}, u32[]{:S(2)}, u32[]{:S(2)}) %collective-permute-start.16) | collective-permute-done | bytes 32800 | tf_op jit(solution)/shard_map/ppermute | solution.py:71
  275.4 5.1 %collective-permute-done.17 = bf16[16,8,128]{2,0,1:T(8,128)(2,1)S(1)} collective-permute-done((bf16[16,8,128]{2,0,1:T(8,128)(2,1)S(1)}, bf16[16,8,128]{2,0,1:T(8,128)(2,1)S(1)}, u32[]{:S(2)}, u32[]{:S(2)}) %collective-permute-start.17) | collective-permute-done | bytes 32800 | tf_op jit(solution)/shard_map/ppermute | solution.py:71
  280.5 5.1 %collective-permute-done.18 = bf16[16,8,128]{2,0,1:T(8,128)(2,1)S(1)} collective-permute-done((bf16[16,8,128]{2,0,1:T(8,128)(2,1)S(1)}, bf16[16,8,128]{2,0,1:T(8,128)(2,1)S(1)}, u32[]{:S(2)}, u32[]{:S(2)}) %collective-permute-start.18) | collective-permute-done | bytes 32800 | tf_op jit(solution)/shard_map/ppermute | solution.py:71
  285.7 5.1 %collective-permute-done.19 = bf16[16,8,128]{2,0,1:T(8,128)(2,1)S(1)} collective-permute-done((bf16[16,8,128]{2,0,1:T(8,128)(2,1)S(1)}, bf16[16,8,128]{2,0,1:T(8,128)(2,1)S(1)}, u32[]{:S(2)}, u32[]{:S(2)}) %collective-permute-start.19) | collective-permute-done | bytes 32800 | tf_op jit(solution)/shard_map/ppermute | solution.py:71
  290.8 5.1 %collective-permute-done.20 = bf16[16,8,128]{2,0,1:T(8,128)(2,1)S(1)} collective-permute-done((bf16[16,8,128]{2,0,1:T(8,128)(2,1)S(1)}, bf16[16,8,128]{2,0,1:T(8,128)(2,1)S(1)}, u32[]{:S(2)}, u32[]{:S(2)}) %collective-permute-start.20) | collective-permute-done | bytes 32800 | tf_op jit(solution)/shard_map/ppermute | solution.py:71
  296.4 19.7 %while.46 = (s32[]{:T(128)}, f32[16,8,128]{2,1,0:T(8,128)S(1)}, s32[]{:T(128)}, s32[128]{0:T(128)S(1)}, s32[128]{0:T(128)S(1)}, /*index=5*/bf16[128,8,128]{2,1,0...) while((s32[]{:T(128)}, f32[16,8,128]{2,1,0:T(8,128)S(1)}, ...), condition=%wide.region_20.22_spmd.clone, body=%wide.region_18.21_spmd.clone.sunk | while | flops 8455462 | bytes 1774899 | solution.py:94
  297.8 1.9 convolution_multiply_fusion.10
  302.7 1.9 convolution_multiply_fusion.10
  307.6 1.9 convolution_multiply_fusion.10
  312.5 1.9 convolution_multiply_fusion.10
  316.1 8.2 %all_to_all.35 = f32[4,4,8,128]{3,2,1,0:T(8,128)S(1)} all-to-all(f32[4,4,8,128]{3,2,1,0:T(8,128)S(1)} %bitcast.218), channel_id=1, replica_groups=mesh['row'=4,'col'=8] {'row'}, dimensions={0} | all-to-all | bytes 131072 | tf_op jit(solution)/shard_map/all_to_all | solution.py:117
  324.6 37.1 %psum.38 = f32[8]{0:T(128)S(1)} all-reduce(f32[8]{0:T(128)S(1)} %get-tuple-element.406), channel_id=1, replica_groups=mesh['row'=4,'col'=8] {'row','col'}, use_global_device_ids=true, to_apply=%region_22.24 | all-reduce | flops 8 | bytes 64 | tf_op jit(solution)/shard_map/psum | solution.py:126
  361.8 5.1 %collective-permute-done.21 = bf16[16,8,128]{2,0,1:T(8,128)(2,1)S(1)} collective-permute-done((bf16[16,8,128]{2,0,1:T(8,128)(2,1)S(1)}, bf16[16,8,128]{2,0,1:T(8,128)(2,1)S(1)}, u32[]{:S(2)}, u32[]{:S(2)}) %collective-permute-start.21) | collective-permute-done | bytes 32800 | tf_op jit(solution)/shard_map/ppermute | solution.py:71
  366.9 5.1 %collective-permute-done.22 = bf16[16,8,128]{2,0,1:T(8,128)(2,1)S(1)} collective-permute-done((bf16[16,8,128]{2,0,1:T(8,128)(2,1)S(1)}, bf16[16,8,128]{2,0,1:T(8,128)(2,1)S(1)}, u32[]{:S(2)}, u32[]{:S(2)}) %collective-permute-start.22) | collective-permute-done | bytes 32800 | tf_op jit(solution)/shard_map/ppermute | solution.py:71
  372.1 5.1 %collective-permute-done.23 = bf16[16,8,128]{2,0,1:T(8,128)(2,1)S(1)} collective-permute-done((bf16[16,8,128]{2,0,1:T(8,128)(2,1)S(1)}, bf16[16,8,128]{2,0,1:T(8,128)(2,1)S(1)}, u32[]{:S(2)}, u32[]{:S(2)}) %collective-permute-start.23) | collective-permute-done | bytes 32800 | tf_op jit(solution)/shard_map/ppermute | solution.py:71
  377.2 5.1 %collective-permute-done.24 = bf16[16,8,128]{2,0,1:T(8,128)(2,1)S(1)} collective-permute-done((bf16[16,8,128]{2,0,1:T(8,128)(2,1)S(1)}, bf16[16,8,128]{2,0,1:T(8,128)(2,1)S(1)}, u32[]{:S(2)}, u32[]{:S(2)}) %collective-permute-start.24) | collective-permute-done | bytes 32800 | tf_op jit(solution)/shard_map/ppermute | solution.py:71
  382.3 5.1 %collective-permute-done.25 = bf16[16,8,128]{2,0,1:T(8,128)(2,1)S(1)} collective-permute-done((bf16[16,8,128]{2,0,1:T(8,128)(2,1)S(1)}, bf16[16,8,128]{2,0,1:T(8,128)(2,1)S(1)}, u32[]{:S(2)}, u32[]{:S(2)}) %collective-permute-start.25) | collective-permute-done | bytes 32800 | tf_op jit(solution)/shard_map/ppermute | solution.py:71
  387.5 5.1 %collective-permute-done.26 = bf16[16,8,128]{2,0,1:T(8,128)(2,1)S(1)} collective-permute-done((bf16[16,8,128]{2,0,1:T(8,128)(2,1)S(1)}, bf16[16,8,128]{2,0,1:T(8,128)(2,1)S(1)}, u32[]{:S(2)}, u32[]{:S(2)}) %collective-permute-start.26) | collective-permute-done | bytes 32800 | tf_op jit(solution)/shard_map/ppermute | solution.py:71
  392.6 5.1 %collective-permute-done.27 = bf16[16,8,128]{2,0,1:T(8,128)(2,1)S(1)} collective-permute-done((bf16[16,8,128]{2,0,1:T(8,128)(2,1)S(1)}, bf16[16,8,128]{2,0,1:T(8,128)(2,1)S(1)}, u32[]{:S(2)}, u32[]{:S(2)}) %collective-permute-start.27) | collective-permute-done | bytes 32800 | tf_op jit(solution)/shard_map/ppermute | solution.py:71
  398.2 19.7 %while.47 = (s32[]{:T(128)}, f32[16,8,128]{2,1,0:T(8,128)S(1)}, s32[]{:T(128)}, s32[128]{0:T(128)S(1)}, s32[128]{0:T(128)S(1)}, /*index=5*/bf16[128,8,128]{2,1,0...) while((s32[]{:T(128)}, f32[16,8,128]{2,1,0:T(8,128)S(1)}, ...), condition=%wide.region_25.27_spmd.clone, body=%wide.region_23.26_spmd.clone.sunk | while | flops 8455462 | bytes 1774899 | solution.py:94
  399.6 1.9 convolution_multiply_fusion.11
  404.5 1.9 convolution_multiply_fusion.11
  409.4 1.9 convolution_multiply_fusion.11
  414.3 1.9 convolution_multiply_fusion.11
  417.9 8.2 %all_to_all.36 = f32[4,4,8,128]{3,2,1,0:T(8,128)S(1)} all-to-all(f32[4,4,8,128]{3,2,1,0:T(8,128)S(1)} %bitcast.216), channel_id=1, replica_groups=mesh['row'=4,'col'=8] {'row'}, dimensions={0} | all-to-all | bytes 131072 | tf_op jit(solution)/shard_map/all_to_all | solution.py:117
  426.4 36.9 %psum.39 = f32[8]{0:T(128)S(1)} all-reduce(f32[8]{0:T(128)S(1)} %get-tuple-element.495), channel_id=1, replica_groups=mesh['row'=4,'col'=8] {'row','col'}, use_global_device_ids=true, to_apply=%region_27.29 | all-reduce | flops 8 | bytes 64 | tf_op jit(solution)/shard_map/psum | solution.py:126
  464.2 41.5 %all-reduce = (f32[1,8]{1,0:T(1,128)S(1)}, f32[1,8]{1,0:T(1,128)S(1)}, f32[1,8]{1,0:T(1,128)S(1)}, f32[1,8]{1,0:T(1,128)S(1)}) all-reduce(f32[1,8]{1,0:T(1,128)S(1)} %bitcast.228, f32[1,8]{1,0:T(1,128)S(1)} %bitcast.227, f32[1,8]{1,0:T(1,128)S(1)} %bitcast.230, f32[1,8]{1,0:T(1,128)S(1)} %bitcast.229), channel_id=1, replica_groups=mesh['row'=4,'col'=8] {'row','col'}, use_global_device_ids=true, to_apply=%region_35.37 | all-reduce | flops 32 | bytes 256 | tf_op jit(solution)/shard_map/pmax | solution.py:128
  (190 shorter events, 54.2 us)
Async XLA Ops:
  0.6 65.4 %copy-start.1 = (s32[1,1,128]{2,1,0:T(1,128)S(1)}, s32[1,1,128]{2,1,0:T(1,128)}, u32[]{:S(2)}) copy-start(s32[1,1,128]{2,1,0:T(1,128)} %param.16) | copy-start | bytes 1540
  0.6 83.9 %copy-start = (s32[1,1,128]{2,1,0:T(1,128)S(1)}, s32[1,1,128]{2,1,0:T(1,128)}, u32[]{:S(2)}) copy-start(s32[1,1,128]{2,1,0:T(1,128)} %param.17) | copy-start | bytes 1540
  44.6 6.1 %collective-permute-start = (bf16[16,8,128]{2,0,1:T(8,128)(2,1)S(1)}, bf16[16,8,128]{2,0,1:T(8,128)(2,1)S(1)}, u32[]{:S(2)}, u32[]{:S(2)}) collective-permute-start(bf16[16,8,128]{2,0,1:T(8,128)(2,1)S(1)} %bitcast.225), channel_id=1, source_target_pairs={{0,1},{1,2},{2,3},{3,4},{4,5},{5,6},{6,7},{7,0},{8,9},{9,10},{10,1... | collective-permute-start | bytes 98312 | tf_op jit(solution)/shard_map/ppermute | solution.py:71
  47.1 30.9 %all-to-all-start = ((s32[4,1,4]{2,1,0:T(1,128)}), s32[4,1,4]{2,1,0:T(1,128)S(1)}, u32[]{:S(2)}, u32[]{:S(2)}) async-start(s32[4,1,4]{2,1,0:T(1,128)} %bitcast.3), calls=%async_computation | async-start | bytes 4096 | tf_op jit(solution)/shard_map/all_to_all | solution.py:103
  50.6 5.1 %collective-permute-start.1 = (bf16[16,8,128]{2,0,1:T(8,128)(2,1)S(1)}, bf16[16,8,128]{2,0,1:T(8,128)(2,1)S(1)}, u32[]{:S(2)}, u32[]{:S(2)}) collective-permute-start(bf16[16,8,128]{2,0,1:T(8,128)(2,1)S(1)} %collective-permute-done), channel_id=1, source_target_pairs={{0,1},{1,2},{2,3},{3,4},{4,5},{5,6},{6,7},{7,0},{8,9},{9,10},{10,1... | collective-permute-start | bytes 98312 | tf_op jit(solution)/shard_map/ppermute | solution.py:71
  55.8 5.1 %collective-permute-start.2 = (bf16[16,8,128]{2,0,1:T(8,128)(2,1)S(1)}, bf16[16,8,128]{2,0,1:T(8,128)(2,1)S(1)}, u32[]{:S(2)}, u32[]{:S(2)}) collective-permute-start(bf16[16,8,128]{2,0,1:T(8,128)(2,1)S(1)} %collective-permute-done.1), channel_id=1, source_target_pairs={{0,1},{1,2},{2,3},{3,4},{4,5},{5,6},{6,7},{7,0},{8,9},{9,10},{10,1... | collective-permute-start | bytes 98312 | tf_op jit(solution)/shard_map/ppermute | solution.py:71
  60.9 5.1 %collective-permute-start.3 = (bf16[16,8,128]{2,0,1:T(8,128)(2,1)S(1)}, bf16[16,8,128]{2,0,1:T(8,128)(2,1)S(1)}, u32[]{:S(2)}, u32[]{:S(2)}) collective-permute-start(bf16[16,8,128]{2,0,1:T(8,128)(2,1)S(1)} %collective-permute-done.2), channel_id=1, source_target_pairs={{0,1},{1,2},{2,3},{3,4},{4,5},{5,6},{6,7},{7,0},{8,9},{9,10},{10,1... | collective-permute-start | bytes 98312 | tf_op jit(solution)/shard_map/ppermute | solution.py:71
  66.1 5.1 %collective-permute-start.4 = (bf16[16,8,128]{2,0,1:T(8,128)(2,1)S(1)}, bf16[16,8,128]{2,0,1:T(8,128)(2,1)S(1)}, u32[]{:S(2)}, u32[]{:S(2)}) collective-permute-start(bf16[16,8,128]{2,0,1:T(8,128)(2,1)S(1)} %collective-permute-done.3), channel_id=1, source_target_pairs={{0,1},{1,2},{2,3},{3,4},{4,5},{5,6},{6,7},{7,0},{8,9},{9,10},{10,1... | collective-permute-start | bytes 98312 | tf_op jit(solution)/shard_map/ppermute | solution.py:71
  71.2 5.1 %collective-permute-start.5 = (bf16[16,8,128]{2,0,1:T(8,128)(2,1)S(1)}, bf16[16,8,128]{2,0,1:T(8,128)(2,1)S(1)}, u32[]{:S(2)}, u32[]{:S(2)}) collective-permute-start(bf16[16,8,128]{2,0,1:T(8,128)(2,1)S(1)} %collective-permute-done.4), channel_id=1, source_target_pairs={{0,1},{1,2},{2,3},{3,4},{4,5},{5,6},{6,7},{7,0},{8,9},{9,10},{10,1... | collective-permute-start | bytes 98312 | tf_op jit(solution)/shard_map/ppermute | solution.py:71
  76.3 7.1 %collective-permute-start.6 = (bf16[16,8,128]{2,0,1:T(8,128)(2,1)S(1)}, bf16[16,8,128]{2,0,1:T(8,128)(2,1)S(1)}, u32[]{:S(2)}, u32[]{:S(2)}) collective-permute-start(bf16[16,8,128]{2,0,1:T(8,128)(2,1)S(1)} %collective-permute-done.5), channel_id=1, source_target_pairs={{0,1},{1,2},{2,3},{3,4},{4,5},{5,6},{6,7},{7,0},{8,9},{9,10},{10,1... | collective-permute-start | bytes 98312 | tf_op jit(solution)/shard_map/ppermute | solution.py:71
  78.0 34.9 %all-to-all-start.2 = ((f32[4,4,1,128]{3,1,2,0:T(4,128)}), f32[4,4,1,128]{3,1,2,0:T(4,128)S(1)}, u32[]{:S(2)}, u32[]{:S(2)}) async-start(f32[4,4,1,128]{3,1,2,0:T(4,128)} %bitcast.14), calls=%async_computation.2 | async-start | bytes 16384 | tf_op jit(solution)/shard_map/all_to_all | solution.py:102
  112.9 8.1 %all-to-all-start.1 = ((f32[4,4,8,128]{3,2,1,0:T(8,128)}), f32[4,4,8,128]{3,2,1,0:T(8,128)S(1)}, u32[]{:S(2)}, u32[]{:S(2)}) async-start(f32[4,4,8,128]{3,2,1,0:T(8,128)} %bitcast.8), calls=%async_computation.1 | async-start | bytes 131072 | tf_op jit(solution)/shard_map/all_to_all | solution.py:101
  158.3 5.2 %collective-permute-start.7 = (bf16[16,8,128]{2,0,1:T(8,128)(2,1)S(1)}, bf16[16,8,128]{2,0,1:T(8,128)(2,1)S(1)}, u32[]{:S(2)}, u32[]{:S(2)}) collective-permute-start(bf16[16,8,128]{2,0,1:T(8,128)(2,1)S(1)} %get-tuple-element.481), channel_id=1, source_target_pairs={{0,1},{1,2},{2,3},{3,4},{4,5},{5,6},{6,7},{7,0},{8,9},{9,10},{10,1... | collective-permute-start | bytes 98312 | tf_op jit(solution)/shard_map/ppermute | solution.py:71
  163.5 5.1 %collective-permute-start.8 = (bf16[16,8,128]{2,0,1:T(8,128)(2,1)S(1)}, bf16[16,8,128]{2,0,1:T(8,128)(2,1)S(1)}, u32[]{:S(2)}, u32[]{:S(2)}) collective-permute-start(bf16[16,8,128]{2,0,1:T(8,128)(2,1)S(1)} %collective-permute-done.7), channel_id=1, source_target_pairs={{0,1},{1,2},{2,3},{3,4},{4,5},{5,6},{6,7},{7,0},{8,9},{9,10},{10,1... | collective-permute-start | bytes 98312 | tf_op jit(solution)/shard_map/ppermute | solution.py:71
  168.6 5.1 %collective-permute-start.9 = (bf16[16,8,128]{2,0,1:T(8,128)(2,1)S(1)}, bf16[16,8,128]{2,0,1:T(8,128)(2,1)S(1)}, u32[]{:S(2)}, u32[]{:S(2)}) collective-permute-start(bf16[16,8,128]{2,0,1:T(8,128)(2,1)S(1)} %collective-permute-done.8), channel_id=1, source_target_pairs={{0,1},{1,2},{2,3},{3,4},{4,5},{5,6},{6,7},{7,0},{8,9},{9,10},{10,1... | collective-permute-start | bytes 98312 | tf_op jit(solution)/shard_map/ppermute | solution.py:71
  173.8 5.1 %collective-permute-start.10 = (bf16[16,8,128]{2,0,1:T(8,128)(2,1)S(1)}, bf16[16,8,128]{2,0,1:T(8,128)(2,1)S(1)}, u32[]{:S(2)}, u32[]{:S(2)}) collective-permute-start(bf16[16,8,128]{2,0,1:T(8,128)(2,1)S(1)} %collective-permute-done.9), channel_id=1, source_target_pairs={{0,1},{1,2},{2,3},{3,4},{4,5},{5,6},{6,7},{7,0},{8,9},{9,10},{10,1... | collective-permute-start | bytes 98312 | tf_op jit(solution)/shard_map/ppermute | solution.py:71
  178.9 5.1 %collective-permute-start.11 = (bf16[16,8,128]{2,0,1:T(8,128)(2,1)S(1)}, bf16[16,8,128]{2,0,1:T(8,128)(2,1)S(1)}, u32[]{:S(2)}, u32[]{:S(2)}) collective-permute-start(bf16[16,8,128]{2,0,1:T(8,128)(2,1)S(1)} %collective-permute-done.10), channel_id=1, source_target_pairs={{0,1},{1,2},{2,3},{3,4},{4,5},{5,6},{6,7},{7,0},{8,9},{9,10},{10,1... | collective-permute-start | bytes 98312 | tf_op jit(solution)/shard_map/ppermute | solution.py:71
  184.1 5.1 %collective-permute-start.12 = (bf16[16,8,128]{2,0,1:T(8,128)(2,1)S(1)}, bf16[16,8,128]{2,0,1:T(8,128)(2,1)S(1)}, u32[]{:S(2)}, u32[]{:S(2)}) collective-permute-start(bf16[16,8,128]{2,0,1:T(8,128)(2,1)S(1)} %collective-permute-done.11), channel_id=1, source_target_pairs={{0,1},{1,2},{2,3},{3,4},{4,5},{5,6},{6,7},{7,0},{8,9},{9,10},{10,1... | collective-permute-start | bytes 98312 | tf_op jit(solution)/shard_map/ppermute | solution.py:71
  189.2 5.1 %collective-permute-start.13 = (bf16[16,8,128]{2,0,1:T(8,128)(2,1)S(1)}, bf16[16,8,128]{2,0,1:T(8,128)(2,1)S(1)}, u32[]{:S(2)}, u32[]{:S(2)}) collective-permute-start(bf16[16,8,128]{2,0,1:T(8,128)(2,1)S(1)} %collective-permute-done.12), channel_id=1, source_target_pairs={{0,1},{1,2},{2,3},{3,4},{4,5},{5,6},{6,7},{7,0},{8,9},{9,10},{10,1... | collective-permute-start | bytes 98312 | tf_op jit(solution)/shard_map/ppermute | solution.py:71
  259.9 5.2 %collective-permute-start.14 = (bf16[16,8,128]{2,0,1:T(8,128)(2,1)S(1)}, bf16[16,8,128]{2,0,1:T(8,128)(2,1)S(1)}, u32[]{:S(2)}, u32[]{:S(2)}) collective-permute-start(bf16[16,8,128]{2,0,1:T(8,128)(2,1)S(1)} %get-tuple-element.479), channel_id=1, source_target_pairs={{0,1},{1,2},{2,3},{3,4},{4,5},{5,6},{6,7},{7,0},{8,9},{9,10},{10,1... | collective-permute-start | bytes 98312 | tf_op jit(solution)/shard_map/ppermute | solution.py:71
  265.1 5.1 %collective-permute-start.15 = (bf16[16,8,128]{2,0,1:T(8,128)(2,1)S(1)}, bf16[16,8,128]{2,0,1:T(8,128)(2,1)S(1)}, u32[]{:S(2)}, u32[]{:S(2)}) collective-permute-start(bf16[16,8,128]{2,0,1:T(8,128)(2,1)S(1)} %collective-permute-done.14), channel_id=1, source_target_pairs={{0,1},{1,2},{2,3},{3,4},{4,5},{5,6},{6,7},{7,0},{8,9},{9,10},{10,1... | collective-permute-start | bytes 98312 | tf_op jit(solution)/shard_map/ppermute | solution.py:71
  270.3 5.1 %collective-permute-start.16 = (bf16[16,8,128]{2,0,1:T(8,128)(2,1)S(1)}, bf16[16,8,128]{2,0,1:T(8,128)(2,1)S(1)}, u32[]{:S(2)}, u32[]{:S(2)}) collective-permute-start(bf16[16,8,128]{2,0,1:T(8,128)(2,1)S(1)} %collective-permute-done.15), channel_id=1, source_target_pairs={{0,1},{1,2},{2,3},{3,4},{4,5},{5,6},{6,7},{7,0},{8,9},{9,10},{10,1... | collective-permute-start | bytes 98312 | tf_op jit(solution)/shard_map/ppermute | solution.py:71
  275.4 5.1 %collective-permute-start.17 = (bf16[16,8,128]{2,0,1:T(8,128)(2,1)S(1)}, bf16[16,8,128]{2,0,1:T(8,128)(2,1)S(1)}, u32[]{:S(2)}, u32[]{:S(2)}) collective-permute-start(bf16[16,8,128]{2,0,1:T(8,128)(2,1)S(1)} %collective-permute-done.16), channel_id=1, source_target_pairs={{0,1},{1,2},{2,3},{3,4},{4,5},{5,6},{6,7},{7,0},{8,9},{9,10},{10,1... | collective-permute-start | bytes 98312 | tf_op jit(solution)/shard_map/ppermute | solution.py:71
  280.5 5.1 %collective-permute-start.18 = (bf16[16,8,128]{2,0,1:T(8,128)(2,1)S(1)}, bf16[16,8,128]{2,0,1:T(8,128)(2,1)S(1)}, u32[]{:S(2)}, u32[]{:S(2)}) collective-permute-start(bf16[16,8,128]{2,0,1:T(8,128)(2,1)S(1)} %collective-permute-done.17), channel_id=1, source_target_pairs={{0,1},{1,2},{2,3},{3,4},{4,5},{5,6},{6,7},{7,0},{8,9},{9,10},{10,1... | collective-permute-start | bytes 98312 | tf_op jit(solution)/shard_map/ppermute | solution.py:71
  285.7 5.1 %collective-permute-start.19 = (bf16[16,8,128]{2,0,1:T(8,128)(2,1)S(1)}, bf16[16,8,128]{2,0,1:T(8,128)(2,1)S(1)}, u32[]{:S(2)}, u32[]{:S(2)}) collective-permute-start(bf16[16,8,128]{2,0,1:T(8,128)(2,1)S(1)} %collective-permute-done.18), channel_id=1, source_target_pairs={{0,1},{1,2},{2,3},{3,4},{4,5},{5,6},{6,7},{7,0},{8,9},{9,10},{10,1... | collective-permute-start | bytes 98312 | tf_op jit(solution)/shard_map/ppermute | solution.py:71
  290.8 5.1 %collective-permute-start.20 = (bf16[16,8,128]{2,0,1:T(8,128)(2,1)S(1)}, bf16[16,8,128]{2,0,1:T(8,128)(2,1)S(1)}, u32[]{:S(2)}, u32[]{:S(2)}) collective-permute-start(bf16[16,8,128]{2,0,1:T(8,128)(2,1)S(1)} %collective-permute-done.19), channel_id=1, source_target_pairs={{0,1},{1,2},{2,3},{3,4},{4,5},{5,6},{6,7},{7,0},{8,9},{9,10},{10,1... | collective-permute-start | bytes 98312 | tf_op jit(solution)/shard_map/ppermute | solution.py:71
  361.7 5.2 %collective-permute-start.21 = (bf16[16,8,128]{2,0,1:T(8,128)(2,1)S(1)}, bf16[16,8,128]{2,0,1:T(8,128)(2,1)S(1)}, u32[]{:S(2)}, u32[]{:S(2)}) collective-permute-start(bf16[16,8,128]{2,0,1:T(8,128)(2,1)S(1)} %get-tuple-element.477), channel_id=1, source_target_pairs={{0,1},{1,2},{2,3},{3,4},{4,5},{5,6},{6,7},{7,0},{8,9},{9,10},{10,1... | collective-permute-start | bytes 98312 | tf_op jit(solution)/shard_map/ppermute | solution.py:71
  366.9 5.1 %collective-permute-start.22 = (bf16[16,8,128]{2,0,1:T(8,128)(2,1)S(1)}, bf16[16,8,128]{2,0,1:T(8,128)(2,1)S(1)}, u32[]{:S(2)}, u32[]{:S(2)}) collective-permute-start(bf16[16,8,128]{2,0,1:T(8,128)(2,1)S(1)} %collective-permute-done.21), channel_id=1, source_target_pairs={{0,1},{1,2},{2,3},{3,4},{4,5},{5,6},{6,7},{7,0},{8,9},{9,10},{10,1... | collective-permute-start | bytes 98312 | tf_op jit(solution)/shard_map/ppermute | solution.py:71
  372.1 5.1 %collective-permute-start.23 = (bf16[16,8,128]{2,0,1:T(8,128)(2,1)S(1)}, bf16[16,8,128]{2,0,1:T(8,128)(2,1)S(1)}, u32[]{:S(2)}, u32[]{:S(2)}) collective-permute-start(bf16[16,8,128]{2,0,1:T(8,128)(2,1)S(1)} %collective-permute-done.22), channel_id=1, source_target_pairs={{0,1},{1,2},{2,3},{3,4},{4,5},{5,6},{6,7},{7,0},{8,9},{9,10},{10,1... | collective-permute-start | bytes 98312 | tf_op jit(solution)/shard_map/ppermute | solution.py:71
  377.2 5.1 %collective-permute-start.24 = (bf16[16,8,128]{2,0,1:T(8,128)(2,1)S(1)}, bf16[16,8,128]{2,0,1:T(8,128)(2,1)S(1)}, u32[]{:S(2)}, u32[]{:S(2)}) collective-permute-start(bf16[16,8,128]{2,0,1:T(8,128)(2,1)S(1)} %collective-permute-done.23), channel_id=1, source_target_pairs={{0,1},{1,2},{2,3},{3,4},{4,5},{5,6},{6,7},{7,0},{8,9},{9,10},{10,1... | collective-permute-start | bytes 98312 | tf_op jit(solution)/shard_map/ppermute | solution.py:71
  382.3 5.1 %collective-permute-start.25 = (bf16[16,8,128]{2,0,1:T(8,128)(2,1)S(1)}, bf16[16,8,128]{2,0,1:T(8,128)(2,1)S(1)}, u32[]{:S(2)}, u32[]{:S(2)}) collective-permute-start(bf16[16,8,128]{2,0,1:T(8,128)(2,1)S(1)} %collective-permute-done.24), channel_id=1, source_target_pairs={{0,1},{1,2},{2,3},{3,4},{4,5},{5,6},{6,7},{7,0},{8,9},{9,10},{10,1... | collective-permute-start | bytes 98312 | tf_op jit(solution)/shard_map/ppermute | solution.py:71
  387.5 5.1 %collective-permute-start.26 = (bf16[16,8,128]{2,0,1:T(8,128)(2,1)S(1)}, bf16[16,8,128]{2,0,1:T(8,128)(2,1)S(1)}, u32[]{:S(2)}, u32[]{:S(2)}) collective-permute-start(bf16[16,8,128]{2,0,1:T(8,128)(2,1)S(1)} %collective-permute-done.25), channel_id=1, source_target_pairs={{0,1},{1,2},{2,3},{3,4},{4,5},{5,6},{6,7},{7,0},{8,9},{9,10},{10,1... | collective-permute-start | bytes 98312 | tf_op jit(solution)/shard_map/ppermute | solution.py:71
  392.6 5.1 %collective-permute-start.27 = (bf16[16,8,128]{2,0,1:T(8,128)(2,1)S(1)}, bf16[16,8,128]{2,0,1:T(8,128)(2,1)S(1)}, u32[]{:S(2)}, u32[]{:S(2)}) collective-permute-start(bf16[16,8,128]{2,0,1:T(8,128)(2,1)S(1)} %collective-permute-done.26), channel_id=1, source_target_pairs={{0,1},{1,2},{2,3},{3,4},{4,5},{5,6},{6,7},{7,0},{8,9},{9,10},{10,1... | collective-permute-start | bytes 98312 | tf_op jit(solution)/shard_map/ppermute | solution.py:71
